TPU v7x, 32 devices: a whole 2x2x4 slice. The times are simulated.
32 devices in a mesh: row: 8 (over z, x), col: 4 (over y, core).
Axes of the slice: x: 2, y: 2, z: 4, core: 2. Of those that a mesh axis runs over, the one named last changes fastest.
Arguments:
- snapshot: bfloat16 [512, 256, 512], P('row', 'col'), may hold values from -6 to 6
- basis_two: bfloat16 [256, 128], P('col'), may hold values from -0.375 to 0.375
- basis_three: bfloat16 [512, 128], replicated, may hold values from -0.25 to 0.25
Outputs:
- gram: float32 [512, 512], P('row', 'col')
All inputs are finite; a program needn't handle non-finite values.
Results may differ from a plain program's by a relative error of at most 0.0017.
Values may be sent and summed in bfloat16 or wider, within the bound.
No kernel may reach another device: no remote copies, remote signals or barrier semaphores. Data moves between devices by JAX's collectives and lax.ppermute only.
A program may use at most 64 MiB of HBM per device.

v0:
```python
import jax
import jax.numpy as jnp
from jax import lax
from jax.sharding import PartitionSpec as P


def on_device(snapshot, basis_two, basis_three):
    cells_one, cells_two, cells_three = snapshot.shape
    ranks_two = basis_two.shape[1]
    ranks_three = basis_three.shape[1]
    inner = jnp.dot(
        snapshot.reshape(cells_one * cells_two, cells_three),
        basis_three,
        preferred_element_type=jnp.float32,
    )
    inner = inner.astype(jnp.bfloat16).reshape(cells_one, cells_two, ranks_three)
    regrouped = lax.all_to_all(inner, "col", split_axis=2, concat_axis=1, tiled=True)
    whole_factor = lax.all_gather(basis_two, "col", axis=0, tiled=True)
    full = jnp.einsum("abr,bq->qar", regrouped, whole_factor, preferred_element_type=jnp.float32)
    rounded = lax.all_to_all(
        full.astype(jnp.bfloat16), "col", split_axis=0, concat_axis=2, tiled=True
    )
    partial_gram = jnp.einsum(
        "qar,qbr->ab",
        rounded,
        lax.all_gather(rounded, "row", axis=1, tiled=True),
        preferred_element_type=jnp.float32,
    )
    summed_gram = lax.psum_scatter(partial_gram, "col", scatter_dimension=1, tiled=True)
    return summed_gram * (1.0 / (ranks_two * ranks_three))


def solution(mesh):
    in_specs = (P("row", "col", None), P("col", None), P())
    out_specs = P("row", "col")
    return jax.shard_map(
        on_device, mesh=mesh, in_specs=in_specs, out_specs=out_specs, check_vma=False
    )
```

profile of v0, /device:TPU:0, one launch (start us, length us, event | category | flops | bytes accessed | tf_op | source)
XLA Modules:
  0.0 165.3 jit_solution(16451007527104671222)
XLA Ops:
  6.5 0.0 copy-start
  6.5 0.9 copy-done
  7.4 3.4 %convolution_convert_fusion = bf16[4096,128]{1,0:T(8,128)(2,1)S(1)} fusion(bf16[4096,512]{1,0:T(8,128)(2,1)} %bitcast.31, bf16[512,128]{1,0:T(8,128)(2,1)S(1)} %copy-done), kind=kOutput, calls=%fused_computation | convolution fusion | flops 537395200 | bytes 5373952 | tf_op jit(solution)/shard_map/dot_general | solution.py:11
  10.9 0.0 copy-start.1
  10.9 3.0 %copy.20 = bf16[64,64,128]{1,0,2:T(8,128)(2,1)S(1)} copy(bf16[64,64,128]{2,1,0:T(8,128)(2,1)S(1)} %bitcast.32) | data formatting | bytes 2097152 | tf_op jit(solution)/shard_map/reshape | solution.py:16
  13.9 2.6 %reshape.10 = bf16[4,2,65536]{2,1,0:T(2,128)(2,1)} reshape(bf16[128,64,64]{2,1,0:T(8,128)(2,1)S(1)} %bitcast.29) | data formatting | bytes 2097152
  16.5 4.3 %all-to-all-start = ((bf16[4,2,65536]{2,1,0:T(2,128)(2,1)}), bf16[4,2,65536]{2,1,0:T(2,128)(2,1)S(1)}, u32[]{:S(2)}, u32[]{:S(2)}) async-start(bf16[4,2,65536]{2,1,0:T(2,128)(2,1)} %reshape.10), calls=%async_computation | async-start | bytes 2097152 | tf_op jit(solution)/shard_map/all_to_all | solution.py:17
  20.8 0.0 all-gather.2.cloned.1.call-start
  20.8 0.0 copy-done.1
  20.8 15.6 %all_gather.6 = bf16[256,128]{1,0:T(8,128)(2,1)S(1)} all-gather(bf16[64,128]{1,0:T(8,128)(2,1)S(1)} %copy-done.1), channel_id=1, replica_groups=mesh['row'=8,'col'=4] {'col'}, dimensions={0}, use_global_device_ids=true | all-gather | bytes 81920 | tf_op jit(solution)/shard_map/all_gather | solution.py:18
  36.4 0.0 all-to-all-done
  36.4 1.4 reshape.11
  37.8 3.0 %copy.22 = bf16[64,4,64,32]{2,1,3,0:T(4,128)(2,1)} copy(bf16[64,4,64,32]{2,0,3,1:T(8,128)(2,1)S(1)} %bitcast.30) | data formatting | bytes 2097152 | tf_op jit(solution)/shard_map/all_to_all | solution.py:17
  40.8 3.5 %all_to_all.29 = bf16[64,256,32]{1,2,0:T(8,128)(2,1)S(1)} reshape(bf16[64,4,64,32]{2,1,3,0:T(4,128)(2,1)} %copy.22) | data formatting | bytes 2097152 | tf_op jit(solution)/shard_map/all_to_all | solution.py:17
  44.3 0.4 fusion
  44.7 1.7 %copy.23 = bf16[128,64,32]{1,2,0:T(8,128)(2,1)S(1)} copy(bf16[128,64,32]{0,2,1:T(8,128)(2,1)S(1)} %fusion) | data formatting | bytes 1048576 | tf_op jit(solution)/shard_map/convert_element_type | solution.py:21
  46.4 0.9 reshape.12
  47.3 11.2 %all_to_all.36 = bf16[4,2,32768]{2,1,0:T(2,128)(2,1)S(1)} all-to-all(bf16[4,2,32768]{2,1,0:T(2,128)(2,1)S(1)} %reshape.12), channel_id=1, replica_groups=mesh['row'=8,'col'=4] {'col'}, dimensions={0} | all-to-all | bytes 1048576 | tf_op jit(solution)/shard_map/all_to_all | solution.py:20
  58.5 0.7 reshape.13
  59.2 0.1 copy.24
  59.4 1.1 copy.25
  60.5 0.0 all-gather.2.cloned.1.call-update
  60.5 0.0 reduce-scatter.2.cloned.1.call-start
  60.6 73.9 %all-gather.2.cloned.1.call-done = bf16[32,512,128]{2,1,0:T(8,128)(2,1)} async-done(((bf16[32,64,128]{2,1,0:T(8,128)(2,1)}), bf16[32,512,128]{2,1,0:T(8,128)(2,1)}) %all-gather.2.cloned.1.call-update) | async-done | bytes 4194320 | tf_op jit(solution)/shard_map/all_gather | solution.py:26
  134.4 4.2 %convolution_bitcast_fusion = f32[64,512]{1,0:T(8,128)} fusion(bf16[32,64,128]{1,2,0:T(8,128)(2,1)S(1)} %bitcast.28, bf16[32,512,128]{2,1,0:T(8,128)(2,1)} %all-gather.2.cloned.1.call-done), kind=kOutput, calls=%fused_computation.3 | convolution fusion | flops 268435456 | bytes 4849664 | tf_op jit(solution)/shard_map/qar,qbr->ab/dot_general | solution.py:23
  138.7 0.0 reduce-scatter.2.cloned.1.call-update
  138.7 18.3 %reduce-scatter.2.cloned.1.call-done = f32[64,128]{1,0:T(8,128)} async-done(((f32[64,512]{1,0:T(8,128)}), f32[64,128]{1,0:T(8,128)}) %reduce-scatter.2.cloned.1.call-update) | async-done | bytes 32784 | tf_op jit(solution)/shard_map/reduce_scatter | solution.py:29
  157.0 1.4 broadcast_multiply_fusion
Async XLA Ops:
  6.5 0.9 copy-start
  10.9 9.9 %copy-start.1 = (bf16[64,128]{1,0:T(8,128)(2,1)S(1)}, bf16[64,128]{1,0:T(8,128)(2,1)}, u32[]{:S(2)}) copy-start(bf16[64,128]{1,0:T(8,128)(2,1)} %param.4) | copy-start | bytes 49156
  16.5 19.9 %all-to-all-start = ((bf16[4,2,65536]{2,1,0:T(2,128)(2,1)}), bf16[4,2,65536]{2,1,0:T(2,128)(2,1)S(1)}, u32[]{:S(2)}, u32[]{:S(2)}) async-start(bf16[4,2,65536]{2,1,0:T(2,128)(2,1)} %reshape.10), calls=%async_computation | async-start | bytes 2097152 | tf_op jit(solution)/shard_map/all_to_all | solution.py:17
  20.8 113.7 %all-gather.2.cloned.1.call-start = ((), (), s32[]{:S(2)}) async-start(), calls=%async_computation.3 | async-start | bytes 4718592 | tf_op jit(solution)/shard_map/all_gather | solution.py:26
  60.5 96.5 %reduce-scatter.2.cloned.1.call-start = ((), (), s32[]{:S(2)}) async-start(), calls=%async_computation.4 | async-start | bytes 163840 | tf_op jit(solution)/shard_map/reduce_scatter | solution.py:29
Sparse Core Ops, SparseCore 0:
  60.6 73.7 all-gather.1
  138.8 18.1 reduce-scatter.1
where the time goes:
time: 166 us; the launch traced here: 165 us
  waiting for transfers between devices  92.3 us (56%)
  blocking collectives  26.8 us (16%)
  local copies, waits for them, and re-layouts  18.9 us (11%)
  between operations  13.5 us (8%)
  matrix products  8.09 us (5%)
  starting transfers between devices  4.3 us (3%)
    all_gather x1, waiting for transfers between devices, on_device(): lax.all_gather(rounded, 'row', axis=1, tiled=True)  73.9 us
    reduce_scatter x1, waiting for transfers between devices, on_device(): lax.psum_scatter(partial_gram, 'col', scatter_dimension=1, tiled=True)  18.3 us
    all_gather x1, blocking collectives, on_device(): whole_factor = lax.all_gather(basis_two, 'col', axis=0, tiled=True)  15.6 us
    all_to_all x1, blocking collectives, on_device(): lax.all_to_all(full.astype(jnp.bfloat16), 'col', split_axis=0, concat_axi...  11.2 us
    unnamed x8, local copies, waits for them, and re-layouts  6.55 us
    all_to_all x2, local copies, waits for them, and re-layouts, on_device(): lax.all_to_all(inner, 'col', split_axis=2, concat_axis=1, tiled=True)  6.45 us
    all_to_all x1, starting transfers between devices, on_device(): lax.all_to_all(inner, 'col', split_axis=2, concat_axis=1, tiled=True)  4.26 us
    dot_general x1, matrix products, on_device(): jnp.einsum('qar,qbr->ab', rounded, lax.all_gather(rounded, 'row', axis=1,...  4.22 us
  transfers between devices with their start and end apart: 3, of which 2 were waited for; matrix products, arithmetic and copies ran while one was open for 0% of the time, Pallas kernels for 0%

commit v1 on v0

--- a/solution.py
+++ b/solution.py
@@ -2,6 +2,22 @@
 import jax.numpy as jnp
 from jax import lax
 from jax.sharding import PartitionSpec as P
+
+
+def ring_product(x, axis, dim, contribution):
+    count, place, span = (lax.axis_size(axis), lax.axis_index(axis), x.shape[dim])
+    right = [(i, (i + 1) % count) for i in range(count)]
+    left = [(i, (i - 1) % count) for i in range(count)]
+    halfway = count // 2
+    from_left = from_right = x
+    total = contribution(x, place * span)
+    for step in range(1, halfway + 1):
+        from_left = lax.ppermute(from_left, axis, right)
+        if step < count - halfway:
+            from_right = lax.ppermute(from_right, axis, left)
+            total = total + contribution(from_right, (place + step) % count * span)
+        total = total + contribution(from_left, (place - step) % count * span)
+    return total
 
 
 def on_device(snapshot, basis_two, basis_three):
@@ -15,8 +31,17 @@
     )
     inner = inner.astype(jnp.bfloat16).reshape(cells_one, cells_two, ranks_three)
     regrouped = lax.all_to_all(inner, "col", split_axis=2, concat_axis=1, tiled=True)
-    whole_factor = lax.all_gather(basis_two, "col", axis=0, tiled=True)
-    full = jnp.einsum("abr,bq->qar", regrouped, whole_factor, preferred_element_type=jnp.float32)
+    full = ring_product(
+        basis_two,
+        "col",
+        0,
+        lambda part, offset: jnp.einsum(
+            "abr,bq->qar",
+            lax.dynamic_slice_in_dim(regrouped, offset, part.shape[0], axis=1),
+            part,
+            preferred_element_type=jnp.float32,
+        ),
+    )
     rounded = lax.all_to_all(
         full.astype(jnp.bfloat16), "col", split_axis=0, concat_axis=2, tiled=True
     )

time: 166 us -> 166 us (level)
  blocking collectives: 26.8 us -> 11.2 us
  waiting for transfers between devices: 92.3 us -> 105 us
  starting transfers between devices: 4.3 us -> 6.16 us
    all_gather x1 -> x0, blocking collectives: 15.6 us -> none  [on_device(): whole_factor = lax.all_gather(basis_two, 'col', axis=0, tiled=True)]
    ppermute x0 -> x3, waiting for transfers between devices: none -> 12.1 us  [the longest x2 12.1 us: ring_product(): from_left = lax.ppermute(from_left, axis, right)]
    ppermute x0 -> x3, starting transfers between devices: none -> 1.86 us  [the longest x1 1.35 us: ring_product(): from_right = lax.ppermute(from_right, axis, left)]
  transfers between devices with their start and end apart: 3 -> 6, of which waited for: 2 -> 4; matrix products, arithmetic and copies ran while one was open for 0% -> 3% of each run, Pallas kernels for 0% -> 0%
where the time goes in v1:
time: 166 us; the launch traced here: 165 us
  waiting for transfers between devices  105 us (63%)
  local copies, waits for them, and re-layouts  18.9 us (11%)
  between operations  13.5 us (8%)
  blocking collectives  11.2 us (7%)
  matrix products  9.09 us (5%)
  starting transfers between devices  6.16 us (4%)
    all_gather x1, waiting for transfers between devices, on_device(): lax.all_gather(rounded, 'row', axis=1, tiled=True)  73.9 us
    reduce_scatter x1, waiting for transfers between devices, on_device(): lax.psum_scatter(partial_gram, 'col', scatter_dimension=1, tiled=True)  18.3 us
    ppermute x2, waiting for transfers between devices, ring_product(): from_left = lax.ppermute(from_left, axis, right)  12.1 us
    all_to_all x1, blocking collectives, on_device(): lax.all_to_all(full.astype(jnp.bfloat16), 'col', split_axis=0, concat_axi...  11.2 us
    unnamed x8, local copies, waits for them, and re-layouts  6.56 us
    all_to_all x2, local copies, waits for them, and re-layouts, on_device(): lax.all_to_all(inner, 'col', split_axis=2, concat_axis=1, tiled=True)  6.43 us
    all_to_all x1, starting transfers between devices, on_device(): lax.all_to_all(inner, 'col', split_axis=2, concat_axis=1, tiled=True)  4.26 us
    dot_general x1, matrix products, on_device(): jnp.einsum('qar,qbr->ab', rounded, lax.all_gather(rounded, 'row', axis=1,...  4.23 us
  transfers between devices with their start and end apart: 6, of which 4 were waited for; matrix products, arithmetic and copies ran while one was open for 3% of the time, Pallas kernels for 0%

profile of v1, /device:TPU:0, one launch (start us, length us, event | category | flops | bytes accessed | tf_op | source)
XLA Modules:
  0.0 165.3 jit_solution(3806480527712715819)
XLA Ops:
  6.5 0.0 copy-start
  6.5 0.9 copy-done
  7.4 3.4 %convolution_convert_fusion = bf16[4096,128]{1,0:T(8,128)(2,1)S(1)} fusion(bf16[4096,512]{1,0:T(8,128)(2,1)} %bitcast.39, bf16[512,128]{1,0:T(8,128)(2,1)S(1)} %copy-done), kind=kOutput, calls=%fused_computation | convolution fusion | flops 537395200 | bytes 5373952 | tf_op jit(solution)/shard_map/dot_general | solution.py:27
  10.9 0.0 copy-start.1
  10.9 3.0 %copy.20 = bf16[64,64,128]{1,0,2:T(8,128)(2,1)S(1)} copy(bf16[64,64,128]{2,1,0:T(8,128)(2,1)S(1)} %bitcast.40) | data formatting | bytes 2097152 | tf_op jit(solution)/shard_map/reshape | solution.py:32
  13.9 2.7 %reshape.13 = bf16[4,2,65536]{2,1,0:T(2,128)(2,1)} reshape(bf16[128,64,64]{2,1,0:T(8,128)(2,1)S(1)} %bitcast.37) | data formatting | bytes 2097152
  16.5 4.3 %all-to-all-start = ((bf16[4,2,65536]{2,1,0:T(2,128)(2,1)}), bf16[4,2,65536]{2,1,0:T(2,128)(2,1)S(1)}, u32[]{:S(2)}, u32[]{:S(2)}) async-start(bf16[4,2,65536]{2,1,0:T(2,128)(2,1)} %reshape.13), calls=%async_computation | async-start | bytes 2097152 | tf_op jit(solution)/shard_map/all_to_all | solution.py:33
  20.8 0.0 all-gather.2.cloned.1.call-start
  20.8 0.0 copy-done.1
  20.8 0.5 collective-permute-start.1
  21.3 1.4 collective-permute-start
  22.7 12.1 %collective-permute-done.1 = bf16[64,128]{1,0:T(8,128)(2,1)S(1)} collective-permute-done((bf16[64,128]{1,0:T(8,128)(2,1)S(1)}, bf16[64,128]{1,0:T(8,128)(2,1)S(1)}, u32[]{:S(2)}, u32[]{:S(2)}) %collective-permute-start.1) | collective-permute-done | bytes 16416 | tf_op jit(solution)/shard_map/ppermute | solution.py:15
  34.8 0.0 collective-permute-start.2
  34.8 0.6 all-to-all-done
  35.4 1.4 reshape.14
  36.8 3.0 %copy.22 = bf16[64,4,64,32]{2,1,3,0:T(4,128)(2,1)} copy(bf16[64,4,64,32]{2,0,3,1:T(8,128)(2,1)S(1)} %bitcast.38) | data formatting | bytes 2097152 | tf_op jit(solution)/shard_map/all_to_all | solution.py:33
  39.8 3.5 %all_to_all.29 = bf16[64,256,32]{1,2,0:T(8,128)(2,1)S(1)} reshape(bf16[64,4,64,32]{2,1,3,0:T(4,128)(2,1)} %copy.22) | data formatting | bytes 2097152 | tf_op jit(solution)/shard_map/all_to_all | solution.py:33
  43.3 0.4 fusion.5
  43.6 0.0 collective-permute-done
  43.7 0.4 convolution_add_fusion.2
  44.0 0.4 convolution_add_fusion.1
  44.4 0.0 collective-permute-done.2
  44.4 0.4 fusion.1
  44.8 1.7 %copy.23 = bf16[128,64,32]{1,2,0:T(8,128)(2,1)S(1)} copy(bf16[128,64,32]{0,2,1:T(8,128)(2,1)S(1)} %fusion.1) | data formatting | bytes 1048576 | tf_op jit(solution)/shard_map/convert_element_type | solution.py:46
  46.5 0.9 reshape.15
  47.3 11.2 %all_to_all.36 = bf16[4,2,32768]{2,1,0:T(2,128)(2,1)S(1)} all-to-all(bf16[4,2,32768]{2,1,0:T(2,128)(2,1)S(1)} %reshape.15), channel_id=1, replica_groups=mesh['row'=8,'col'=4] {'col'}, dimensions={0} | all-to-all | bytes 1048576 | tf_op jit(solution)/shard_map/all_to_all | solution.py:45
  58.5 0.7 reshape.16
  59.3 0.1 copy.24
  59.4 1.1 copy.25
  60.5 0.0 all-gather.2.cloned.1.call-update
  60.6 0.0 reduce-scatter.2.cloned.1.call-start
  60.6 73.9 %all-gather.2.cloned.1.call-done = bf16[32,512,128]{2,1,0:T(8,128)(2,1)} async-done(((bf16[32,64,128]{2,1,0:T(8,128)(2,1)}), bf16[32,512,128]{2,1,0:T(8,128)(2,1)}) %all-gather.2.cloned.1.call-update) | async-done | bytes 4194320 | tf_op jit(solution)/shard_map/all_gather | solution.py:51
  134.5 4.2 %convolution_bitcast_fusion = f32[64,512]{1,0:T(8,128)} fusion(bf16[32,64,128]{1,2,0:T(8,128)(2,1)S(1)} %bitcast.36, bf16[32,512,128]{2,1,0:T(8,128)(2,1)} %all-gather.2.cloned.1.call-done), kind=kOutput, calls=%fused_computation.6 | convolution fusion | flops 268435456 | bytes 4849664 | tf_op jit(solution)/shard_map/qar,qbr->ab/dot_general | solution.py:48
  138.7 0.0 reduce-scatter.2.cloned.1.call-update
  138.8 18.3 %reduce-scatter.2.cloned.1.call-done = f32[64,128]{1,0:T(8,128)} async-done(((f32[64,512]{1,0:T(8,128)}), f32[64,128]{1,0:T(8,128)}) %reduce-scatter.2.cloned.1.call-update) | async-done | bytes 32784 | tf_op jit(solution)/shard_map/reduce_scatter | solution.py:54
  157.1 1.4 broadcast_multiply_fusion
Async XLA Ops:
  6.5 0.9 copy-start
  10.9 9.9 %copy-start.1 = (bf16[64,128]{1,0:T(8,128)(2,1)S(1)}, bf16[64,128]{1,0:T(8,128)(2,1)}, u32[]{:S(2)}) copy-start(bf16[64,128]{1,0:T(8,128)(2,1)} %param.4) | copy-start | bytes 49156
  16.5 18.9 %all-to-all-start = ((bf16[4,2,65536]{2,1,0:T(2,128)(2,1)}), bf16[4,2,65536]{2,1,0:T(2,128)(2,1)S(1)}, u32[]{:S(2)}, u32[]{:S(2)}) async-start(bf16[4,2,65536]{2,1,0:T(2,128)(2,1)} %reshape.13), calls=%async_computation | async-start | bytes 2097152 | tf_op jit(solution)/shard_map/all_to_all | solution.py:33
  20.8 113.7 %all-gather.2.cloned.1.call-start = ((), (), s32[]{:S(2)}) async-start(), calls=%async_computation.3 | async-start | bytes 4718592 | tf_op jit(solution)/shard_map/all_gather | solution.py:51
  20.8 14.0 %collective-permute-start.1 = (bf16[64,128]{1,0:T(8,128)(2,1)S(1)}, bf16[64,128]{1,0:T(8,128)(2,1)S(1)}, u32[]{:S(2)}, u32[]{:S(2)}) collective-permute-start(bf16[64,128]{1,0:T(8,128)(2,1)S(1)} %copy-done.1), channel_id=1, source_target_pairs={{0,1},{1,2},{2,3},{3,0},{4,5},{5,6},{6,7},{7,4},{8,9},{9,10},{10,1... | collective-permute-start | bytes 49160 | tf_op jit(solution)/shard_map/ppermute | solution.py:15
  21.3 22.3 %collective-permute-start = (bf16[64,128]{1,0:T(8,128)(2,1)S(1)}, bf16[64,128]{1,0:T(8,128)(2,1)S(1)}, u32[]{:S(2)}, u32[]{:S(2)}) collective-permute-start(bf16[64,128]{1,0:T(8,128)(2,1)S(1)} %copy-done.1), channel_id=1, source_target_pairs={{0,3},{1,0},{2,1},{3,2},{4,7},{5,4},{6,5},{7,6},{8,11},{9,8},{10,9... | collective-permute-start | bytes 49160 | tf_op jit(solution)/shard_map/ppermute | solution.py:17
  34.8 9.6 %collective-permute-start.2 = (bf16[64,128]{1,0:T(8,128)(2,1)S(1)}, bf16[64,128]{1,0:T(8,128)(2,1)S(1)}, u32[]{:S(2)}, u32[]{:S(2)}) collective-permute-start(bf16[64,128]{1,0:T(8,128)(2,1)S(1)} %collective-permute-done.1), channel_id=1, source_target_pairs={{0,1},{1,2},{2,3},{3,0},{4,5},{5,6},{6,7},{7,4},{8,9},{9,10},{10,1... | collective-permute-start | bytes 49160 | tf_op jit(solution)/shard_map/ppermute | solution.py:15
  60.6 96.5 %reduce-scatter.2.cloned.1.call-start = ((), (), s32[]{:S(2)}) async-start(), calls=%async_computation.4 | async-start | bytes 163840 | tf_op jit(solution)/shard_map/reduce_scatter | solution.py:54
Sparse Core Ops, SparseCore 0:
  60.7 73.7 all-gather.1
  138.9 18.1 reduce-scatter.1
